TPU v7x, 32 devices: a whole 2x2x4 slice. The times are simulated.
32 devices in a mesh: grp: 4 (over y, x), dom: 8 (over z, core).
Axes of the slice: x: 2, y: 2, z: 4, core: 2. Of those that a mesh axis runs over, the one named last changes fastest.
Arguments:
- fields: float32 [210, 32768], P(None, ('grp', 'dom')), may hold values from -6 to 6
- metric: float32 [9, 32768], P(None, ('grp', 'dom')), may hold values from -5 to 5
- normals: float32 [12, 32768], P(None, ('grp', 'dom')), may hold values from -3 to 3
- fscale: float32 [4, 32768], P(None, ('grp', 'dom')), may hold values from 0.5 to 4
- orders: int32 [32768], P(('grp', 'dom')), may hold values from 1 to 4, as said below
- slots: int32 [32768], P(('grp', 'dom')), may hold values from 0 to 511, as said below
- send_faces: int32 [294912], P(('grp', 'dom')), may hold values from 0 to 8192, as said below
- recv_faces: int32 [262144], P(('grp', 'dom')), may hold values from 0 to 9216, as said below
- dmat: float32 [4, 105, 35], P('grp'), may hold values from -4 to 4
- tmat: float32 [4, 60, 35], P('grp'), may hold values from -4 to 4
- lmat: float32 [4, 35, 60], P('grp'), may hold values from -3 to 3
Outputs:
- rhs: float32 [210, 65536], P(None, ('grp', 'dom'))
Inputs may be any that keep to these rules, and one draw needn't show every extreme that they name: `orders`: on each device every order from 1 to 4 is held by at least one element and by at most 512; one order is held by exactly 512. The elements of one device that share an order have distinct slots. `send_faces`: each entry names a face of an occupied slot of the sending bucket or equals 4 * 2048 (nothing); in each list the items in use stand first. `recv_faces`: every face of an occupied slot names a distinct received item that is in use, and every item in use is named by exactly one face; faces of empty slots hold 9216. A list carries at most 768 items in use, and some list carries exactly 768.
All inputs are finite; a program needn't handle non-finite values.
Results may differ from a plain program's by a relative error of at most 0.0003.
Values sent between devices are 32-bit elements; how exact they have to be, the bound alone decides.
A program may use at most 128 MiB of HBM per device.

v0:
```python
import jax
import jax.numpy as jnp
from jax import lax
from jax.sharding import PartitionSpec as P

NPM = 35
FPTS = 15
exact_prec = lax.Precision.HIGHEST


def shifted(x, axis, by):
    size = lax.axis_size(axis)
    return lax.ppermute(x, axis, [(i, (i + by) % size) for i in range(size)])


def order_mask(order_index):
    node_total = (order_index + 2) * (order_index + 3) * (order_index + 4) // 6
    return (jnp.arange(NPM, dtype=jnp.int32) < node_total).astype(jnp.float32)


def cross_of(first_vec, second_vec):
    return [
        first_vec[1] * second_vec[2] - first_vec[2] * second_vec[1],
        first_vec[2] * second_vec[0] - first_vec[0] * second_vec[2],
        first_vec[0] * second_vec[1] - first_vec[1] * second_vec[0],
    ]


def volume_terms(coefficients, metric_cols, deriv_mats):
    derived = jnp.einsum("anm,qms->qans", deriv_mats, coefficients, precision=exact_prec)

    def partial_of(component, direction):
        return (
            metric_cols[0, direction][None] * derived[component, 0]
            + metric_cols[1, direction][None] * derived[component, 1]
            + metric_cols[2, direction][None] * derived[component, 2]
        )

    curl_h = [
        partial_of(5, 1) - partial_of(4, 2),
        partial_of(3, 2) - partial_of(5, 0),
        partial_of(4, 0) - partial_of(3, 1),
    ]
    curl_e = [
        partial_of(2, 1) - partial_of(1, 2),
        partial_of(0, 2) - partial_of(2, 0),
        partial_of(1, 0) - partial_of(0, 1),
    ]
    return jnp.stack(curl_h + [-value for value in curl_e], 0)


def face_flux(own_traces, neighbour, normal_cols, scale_cols):
    own_split = own_traces.reshape(6, FPTS, -1)
    far_split = neighbour.reshape(6, FPTS, -1)
    jump_e = [far_split[c] - own_split[c] for c in range(3)]
    jump_h = [far_split[c + 3] - own_split[c + 3] for c in range(3)]
    normal = [normal_cols[c] for c in range(3)]
    normal_e = normal[0] * jump_e[0] + normal[1] * jump_e[1] + normal[2] * jump_e[2]
    normal_h = normal[0] * jump_h[0] + normal[1] * jump_h[1] + normal[2] * jump_h[2]
    turn_h = cross_of(normal, jump_h)
    turn_e = cross_of(normal, jump_e)
    flux_e = [0.5 * scale_cols * (turn_h[c] + jump_e[c] - normal[c] * normal_e) for c in range(3)]
    flux_h = [0.5 * scale_cols * (-turn_e[c] + jump_h[c] - normal[c] * normal_h) for c in range(3)]
    return jnp.stack(flux_e + flux_h, 0)


def block_rhs(bucket, own_traces, neighbour, deriv_mats, lift_mat):
    slot_count = bucket.shape[1]
    coefficients = bucket[: 6 * NPM].reshape(6, NPM, slot_count)
    metric_cols = bucket[6 * NPM : 6 * NPM + 9].reshape(3, 3, slot_count)
    normal_cols = bucket[6 * NPM + 9 : 6 * NPM + 21].reshape(3, 1, 4 * slot_count)
    scale_cols = bucket[6 * NPM + 21 : 6 * NPM + 25].reshape(1, 4 * slot_count)
    volume = volume_terms(coefficients, metric_cols, deriv_mats)
    flux = face_flux(own_traces, neighbour, normal_cols, scale_cols).reshape(
        6, FPTS * 4, slot_count
    )
    lifted = jnp.einsum("mp,qps->qms", lift_mat, flux, precision=exact_prec)
    return (volume + lifted).reshape(6 * NPM, slot_count)


def across_groups(outgoing):
    return lax.all_to_all(outgoing, "grp", split_axis=1, concat_axis=1, tiled=True)


def across_columns(outgoing):
    lowered = shifted(outgoing[0], "dom", -1)
    raised = shifted(outgoing[2], "dom", 1)
    return jnp.stack([lowered, outgoing[1], raised], 0)


def local(fields, metric, normals, fscale, orders, slots, send_faces, recv_faces, dmat, tmat, lmat):
    own_group = lax.axis_index("grp")
    groups = lax.axis_size("grp")
    elements = fields.shape[1]
    capacity = elements // 2
    slot_count = groups * capacity
    payload = jnp.concatenate([fields, metric, normals, fscale], 0)
    row_count = payload.shape[0]
    zero_column = jnp.zeros((row_count, 1), jnp.float32)
    target = (orders - 1) * capacity + slots
    inverse = (
        jnp.full((slot_count,), elements, jnp.int32)
        .at[target]
        .set(jnp.arange(elements, dtype=jnp.int32))
    )
    padded = jnp.concatenate([payload, zero_column], 1)
    outgoing = jnp.take(padded, inverse, axis=1).reshape(row_count, groups, capacity)
    bucket = lax.all_to_all(outgoing, "grp", split_axis=1, concat_axis=1, tiled=True).reshape(
        row_count, slot_count
    )
    node_mask = order_mask(own_group)
    deriv_mats = dmat[0].reshape(3, NPM, NPM) * node_mask[None, :, None] * node_mask[None, None, :]
    trace_mat = tmat[0] * node_mask[None, :]
    lift_mat = lmat[0] * node_mask[:, None]
    coefficients = bucket[: 6 * NPM].reshape(6, NPM, slot_count)
    own_traces = jnp.einsum("pm,qms->qps", trace_mat, coefficients, precision=exact_prec).reshape(
        6 * FPTS, 4 * slot_count
    )
    face_rows = jnp.concatenate([own_traces.T, jnp.zeros((1, 6 * FPTS), jnp.float32)], 0)
    list_total = send_faces.shape[0]
    list_size = list_total // (3 * groups)
    outgoing_faces = jnp.take(face_rows, send_faces, axis=0).reshape(3, groups, list_size, 6 * FPTS)
    arrived = across_columns(across_groups(outgoing_faces))
    received = jnp.concatenate(
        [arrived.reshape(list_total, 6 * FPTS), jnp.zeros((1, 6 * FPTS), jnp.float32)], 0
    )
    neighbour = jnp.take(received, recv_faces, axis=0).T
    return block_rhs(bucket, own_traces, neighbour, deriv_mats, lift_mat)


def solution(mesh):
    in_specs = (
        P(None, ("grp", "dom")),
        P(None, ("grp", "dom")),
        P(None, ("grp", "dom")),
        P(None, ("grp", "dom")),
        P(("grp", "dom")),
        P(("grp", "dom")),
        P(("grp", "dom")),
        P(("grp", "dom")),
        P("grp", None, None),
        P("grp", None, None),
        P("grp", None, None),
    )
    out_specs = P(None, ("grp", "dom"))
    return jax.shard_map(local, mesh=mesh, in_specs=in_specs, out_specs=out_specs, check_vma=False)
```

profile of v0, /device:TPU:1, one launch (start us, length us, event | category | flops | bytes accessed | tf_op | source)
XLA Modules:
  0.0 281.7 jit_solution(4036362159378918942)
XLA Ops:
  0.7 4.3 %scatter_custom_fusion = s32[2048]{0:T(1024)S(1)} fusion(s32[1024]{0:T(1024)S(1)} %compare_select_fusion.3, s32[1024]{0:T(1024)S(1)} %iota.14, s32[]{:T(128)} %constant.33.clone.1), kind=kCustom, calls=%fused_computation.79 | custom fusion | bytes 8196 | tf_op jit(solution)/shard_map/scatter | solution.py:104
  11.3 6.6 %gather_fusion = f32[2048,235]{1,0:T(8,128)S(1)} fusion(f32[235,1025]{0,1:T(8,128)S(1)} %select_maximum_fusion, s32[2048]{0:T(1024)S(1)} %fusion.11), kind=kCustom, calls=%fused_computation | custom fusion | bytes 3858432 | tf_op jit(solution)/shard_map/jit(_take)/gather | solution.py:107
  19.8 3.1 %broadcast_select_fusion.1 = f32[235,4,512]{2,0,1:T(8,128)} fusion(f32[235,4,512]{2,0,1:T(8,128)} %copy.62, pred[4,512]{1,0:T(4,128)(4,1)S(1)} %broadcast_in_dim.53), kind=kLoop, calls=%fused_computation.20 | loop fusion | flops 481280 | bytes 3852288 | tf_op jit(solution)/shard_map/jit(_take)/select_n | solution.py:107
  22.9 4.4 %all-to-all-start = ((f32[235,4,512]{2,0,1:T(8,128)}), f32[235,4,512]{2,0,1:T(8,128)S(1)}, u32[]{:S(2)}, u32[]{:S(2)}) async-start(f32[235,4,512]{2,0,1:T(8,128)} %broadcast_select_fusion.1), calls=%async_computation | async-start | bytes 3932160 | tf_op jit(solution)/shard_map/all_to_all | solution.py:108
  29.8 20.6 %all-to-all-done = f32[235,4,512]{2,0,1:T(8,128)S(1)} async-done(((f32[235,4,512]{2,0,1:T(8,128)}), f32[235,4,512]{2,0,1:T(8,128)S(1)}, u32[]{:S(2)}, u32[]{:S(2)}) %all-to-all-start) | async-done | bytes 1925152 | tf_op jit(solution)/shard_map/all_to_all | solution.py:108
  52.9 2.5 reshape.2020
  55.4 2.6 reshape.2060
  58.0 4.7 %convolution_bitcast_fusion.1 = f32[6,60,2048]{2,1,0:T(8,128)S(1)} fusion(f32[6,35,2048]{2,1,0:T(8,128)} %reshape.2020, f32[1,60,35]{1,0,2:T(1,128)S(1)} %broadcast_multiply_fusion), kind=kOutput, calls=%fused_computation.7 | convolution fusion | flops 309657600 | bytes 4677840 | tf_op jit(solution)/shard_map/pm,qms->qps/dot_general | solution.py:116
  62.7 3.0 %reshape.2021 = f32[90,8192]{1,0:T(8,128)} reshape(f32[6,60,2048]{2,1,0:T(8,128)S(1)} %convolution_bitcast_fusion.1) | data formatting | bytes 5898240 | tf_op jit(solution)/shard_map/reshape | solution.py:116
  65.7 5.2 %copy.67 = f32[90,8192]{0,1:T(8,128)} copy(f32[90,8192]{1,0:T(8,128)} %reshape.2021) | data formatting | bytes 5898240 | tf_op jit(solution)/shard_map/reshape | solution.py:116
  70.8 3.8 %concatenate.15 = f32[8193,90]{1,0:T(8,128)} pad(f32[8192,90]{1,0:T(8,128)} %bitcast.170, f32[]{:T(128)} %constant.45.clone.1), padding=0_1x0_0 | pad | bytes 5898604 | tf_op jit(solution)/shard_map/concatenate | solution.py:119
  74.6 33.3 %gather_fusion.1 = f32[9216,90]{1,0:T(8,128)} fusion(f32[8193,90]{1,0:T(8,128)} %concatenate.15, s32[9216]{0:T(1024)S(1)} %fusion.3), kind=kCustom, calls=%fused_computation.1 | custom fusion | bytes 6672384 | tf_op jit(solution)/shard_map/jit(_take)/gather | solution.py:122
  107.9 3.9 %copy.68 = f32[3,4,768,90]{2,3,0,1:T(8,128)S(1)} copy(f32[3,4,768,90]{3,2,1,0:T(8,128)} %bitcast.168) | data formatting | bytes 6635520 | tf_op jit(solution)/shard_map/jit(_take)/gather | solution.py:122
  114.1 4.0 %all-to-all-start.1 = ((f32[3,4,768,90]{2,3,0,1:T(8,128)}), f32[3,4,768,90]{2,3,0,1:T(8,128)S(1)}, u32[]{:S(2)}, u32[]{:S(2)}) async-start(f32[3,4,768,90]{2,3,0,1:T(8,128)} %broadcast_select_fusion), calls=%async_computation.1 | async-start | bytes 7077888 | tf_op jit(solution)/shard_map/all_to_all | solution.py:82
  118.0 10.5 %convolution_bitcast_fusion = f32[6,3,35,2048]{3,2,1,0:T(8,128)} fusion(f32[6,35,2048,1]{2,1,0,3:T(8,128)} %reshape.2060, f32[3,35,35]{2,1,0:T(8,128)} %copy.65), kind=kOutput, calls=%fused_computation.5 | convolution fusion | flops 541900800 | bytes 6895980 | tf_op jit(solution)/shard_map/anm,qms->qans/dot_general | solution.py:30
  142.4 15.2 %all-to-all-done.1 = f32[3,4,768,90]{2,3,0,1:T(8,128)S(1)} async-done(((f32[3,4,768,90]{2,3,0,1:T(8,128)}), f32[3,4,768,90]{2,3,0,1:T(8,128)S(1)}, u32[]{:S(2)}, u32[]{:S(2)}) %all-to-all-start.1) | async-done | bytes 3317792 | tf_op jit(solution)/shard_map/all_to_all | solution.py:82
  159.5 2.7 collective-permute-start.1
  174.3 7.7 %collective-permute-done.1 = f32[4,768,90]{1,0,2:T(4,128)S(1)} collective-permute-done((f32[4,768,90]{1,0,2:T(4,128)S(1)}, f32[4,768,90]{1,0,2:T(4,128)S(1)}, u32[]{:S(2)}, u32[]{:S(2)}) %collective-permute-start.1) | collective-permute-done | bytes 1105952 | tf_op jit(solution)/shard_map/ppermute | solution.py:13
  182.3 6.7 %collective-permute-done = f32[4,768,90]{1,0,2:T(4,128)} collective-permute-done((f32[4,768,90]{1,0,2:T(4,128)}, f32[4,768,90]{1,0,2:T(4,128)}, u32[]{:S(2)}, u32[]{:S(2)}) %collective-permute-start) | collective-permute-done | bytes 1105952 | tf_op jit(solution)/shard_map/ppermute | solution.py:13
  190.7 3.6 %copy.73 = f32[3,4,768,90]{3,2,1,0:T(8,128)} copy(f32[3,4,768,90]{2,3,0,1:T(8,128)S(1)} %pad_maximum_fusion) | data formatting | bytes 6635520 | tf_op jit(solution)/shard_map/stack | solution.py:88
  194.3 4.0 %concatenate.16 = f32[9217,90]{1,0:T(8,128)} pad(f32[9216,90]{1,0:T(8,128)} %bitcast.169, f32[]{:T(128)} %constant.45.clone.1), padding=0_1x0_0 | pad | bytes 6635884 | tf_op jit(solution)/shard_map/concatenate | solution.py:124
  198.3 30.1 %gather_fusion.2 = f32[8192,90]{1,0:T(8,128)} fusion(f32[9217,90]{1,0:T(8,128)} %concatenate.16, s32[8192]{0:T(1024)S(1)} %copy-done.25), kind=kCustom, calls=%fused_computation.2 | custom fusion | bytes 5931008 | tf_op jit(solution)/shard_map/jit(_take)/gather | solution.py:127
  228.4 6.2 %select_bitcast_fusion = f32[90,8192]{0,1:T(8,128)S(1)} fusion(f32[8192,90]{1,0:T(8,128)} %gather_fusion.2, pred[8192]{0:T(1024)(128)(4,1)S(1)} %copy-done.26), kind=kLoop, calls=%fused_computation.4 | loop fusion | flops 737280 | bytes 5906432 | tf_op jit(solution)/shard_map/jit(_take)/select_n | solution.py:127
  234.6 11.1 %fusion.14 = (f32[15,8192]{0,1:T(8,128)}, f32[15,8192]{0,1:T(8,128)}, f32[15,8192]{0,1:T(8,128)}, f32[15,8192]{0,1:T(8,128)}, f32[15,8192]{0,1:T(8,128)}, /*index=5*/f32[15,8192]{0,1:T(8,128)}) fusion(f32[90,8192]{0,1:T(8,128)S(1)} %select_bitcast_fusion), kind=kLoop, calls=%fused_computation.82 | loop fusion | bytes 5898240 | tf_op jit(solution)/shard_map/slice | solution.py:56
  245.7 2.8 %copy.74 = f32[15,8192]{1,0:T(8,128)S(1)} copy(f32[15,8192]{0,1:T(8,128)} %get-tuple-element.18) | data formatting | bytes 983040 | tf_op jit(solution)/shard_map/slice | solution.py:56
  249.5 2.8 %copy.75 = f32[15,8192]{1,0:T(8,128)S(1)} copy(f32[15,8192]{0,1:T(8,128)} %get-tuple-element.17) | data formatting | bytes 983040 | tf_op jit(solution)/shard_map/slice | solution.py:56
  253.3 2.8 %copy.76 = f32[15,8192]{1,0:T(8,128)S(1)} copy(f32[15,8192]{0,1:T(8,128)} %get-tuple-element.16) | data formatting | bytes 983040 | tf_op jit(solution)/shard_map/slice | solution.py:55
  257.1 2.8 %copy.77 = f32[15,8192]{1,0:T(8,128)S(1)} copy(f32[15,8192]{0,1:T(8,128)} %get-tuple-element.15) | data formatting | bytes 983040 | tf_op jit(solution)/shard_map/slice | solution.py:55
  260.9 2.8 %copy.78 = f32[15,8192]{1,0:T(8,128)S(1)} copy(f32[15,8192]{0,1:T(8,128)} %get-tuple-element.14) | data formatting | bytes 983040 | tf_op jit(solution)/shard_map/slice | solution.py:55
  264.7 3.7 %copy.79 = f32[15,8192]{1,0:T(8,128)} copy(f32[15,8192]{0,1:T(8,128)} %get-tuple-element.13) | data formatting | bytes 983040 | tf_op jit(solution)/shard_map/slice | solution.py:56
  270.4 3.2 %multiply_dynamic-update-slice_fusion.5 = (f32[6,60,2048]{2,1,0:T(8,128)S(1)}, f32[1,60,2048]{2,1,0:T(8,128)S(1)}, f32[1,60,2048]{2,1,0:T(8,128)S(1)}, f32[1,60,...) fusion(f32[1,60,2048]{2,1,0:T(8,128)} %mul.929, f32[1,60,2048]{2,1,0:T(8,128)} %mul.943, ...), kind=kLoop, calls=%fused_computation.33 | loop fusion | flops 2088959 | bytes 10027008
  276.1 4.2 %fusion = f32[6,35,2048]{2,1,0:T(8,128)S(1)} fusion(f32[6,35,2048]{2,1,0:T(8,128)} %negate_dynamic-update-slice_fusion, f32[6,60,2048]{2,1,0:T(8,128)S(1)} %multiply_dynamic-update-slice_fusion, f32[1,35,60]{2,0,1:T(1,128)S(1)} %copy-done.27, f32[35]{0:T(128)S(1)} %copy-done.32), kind=kOutput, calls=%fused_computation.9 | convolution fusion | flops 310089792 | bytes 6398300 | tf_op jit(solution)/shard_map/mp,qps->qms/dot_general | solution.py:77
  (131 shorter events, 56.2 us)
Async XLA Ops:
  0.0 8.7 %copy-start.30 = (f32[4,1024]{1,0:T(4,128)S(1)}, f32[4,1024]{1,0:T(4,128)}, u32[]{:S(2)}) copy-start(f32[4,1024]{1,0:T(4,128)} %param.14) | copy-start | bytes 49156
  19.7 7.6 %copy-start.23 = (s32[9216]{0:T(1024)S(1)}, s32[9216]{0:T(1024)}, u32[]{:S(2)}) copy-start(s32[9216]{0:T(1024)} %param.17) | copy-start | bytes 110596
  19.7 7.8 %copy-start.28 = (f32[1,105,35]{1,0,2:T(1,128)S(1)}, f32[1,105,35]{1,0,2:T(1,128)}, u32[]{:S(2)}) copy-start(f32[1,105,35]{1,0,2:T(1,128)} %param.19) | copy-start | bytes 44104
  19.8 8.7 %copy-start.29 = (f32[1,60,35]{1,0,2:T(1,128)S(1)}, f32[1,60,35]{1,0,2:T(1,128)}, u32[]{:S(2)}) copy-start(f32[1,60,35]{1,0,2:T(1,128)} %param.20) | copy-start | bytes 25204
  22.9 5.7 %copy-start.24 = (s32[8192]{0:T(1024)S(1)}, s32[8192]{0:T(1024)}, u32[]{:S(2)}) copy-start(s32[8192]{0:T(1024)} %param.18) | copy-start | bytes 98308
  22.9 27.5 %all-to-all-start = ((f32[235,4,512]{2,0,1:T(8,128)}), f32[235,4,512]{2,0,1:T(8,128)S(1)}, u32[]{:S(2)}, u32[]{:S(2)}) async-start(f32[235,4,512]{2,0,1:T(8,128)} %broadcast_select_fusion.1), calls=%async_computation | async-start | bytes 3932160 | tf_op jit(solution)/shard_map/all_to_all | solution.py:108
  27.4 25.5 %copy-start.31 = (f32[35]{0:T(128)}, f32[35]{0:T(128)S(1)}, u32[]{:S(2)}) copy-start(f32[35]{0:T(128)S(1)} %compare_convert_fusion) | copy-start | bytes 424
  114.1 43.5 %all-to-all-start.1 = ((f32[3,4,768,90]{2,3,0,1:T(8,128)}), f32[3,4,768,90]{2,3,0,1:T(8,128)S(1)}, u32[]{:S(2)}, u32[]{:S(2)}) async-start(f32[3,4,768,90]{2,3,0,1:T(8,128)} %broadcast_select_fusion), calls=%async_computation.1 | async-start | bytes 7077888 | tf_op jit(solution)/shard_map/all_to_all | solution.py:82
  132.8 7.2 %copy-start.9 = (f32[1,1,2048]{2,1,0:T(1,128)}, f32[1,1,2048]{2,1,0:T(1,128)S(1)}, u32[]{:S(2)}) copy-start(f32[1,1,2048]{2,1,0:T(1,128)S(1)} %get-tuple-element.28) | copy-start | bytes 24580
  132.8 7.2 %copy-start.11 = (f32[1,1,2048]{2,1,0:T(1,128)}, f32[1,1,2048]{2,1,0:T(1,128)S(1)}, u32[]{:S(2)}) copy-start(f32[1,1,2048]{2,1,0:T(1,128)S(1)} %get-tuple-element.32) | copy-start | bytes 24580
  132.8 7.2 %copy-start.13 = (f32[1,1,2048]{2,1,0:T(1,128)}, f32[1,1,2048]{2,1,0:T(1,128)S(1)}, u32[]{:S(2)}) copy-start(f32[1,1,2048]{2,1,0:T(1,128)S(1)} %get-tuple-element.33) | copy-start | bytes 24580
  132.8 7.2 %copy-start.15 = (f32[1,1,2048]{2,1,0:T(1,128)}, f32[1,1,2048]{2,1,0:T(1,128)S(1)}, u32[]{:S(2)}) copy-start(f32[1,1,2048]{2,1,0:T(1,128)S(1)} %get-tuple-element.34) | copy-start | bytes 24580
  132.8 7.2 %copy-start.17 = (f32[1,1,2048]{2,1,0:T(1,128)}, f32[1,1,2048]{2,1,0:T(1,128)S(1)}, u32[]{:S(2)}) copy-start(f32[1,1,2048]{2,1,0:T(1,128)S(1)} %get-tuple-element.29) | copy-start | bytes 24580
  132.8 7.2 %copy-start.19 = (f32[1,1,2048]{2,1,0:T(1,128)}, f32[1,1,2048]{2,1,0:T(1,128)S(1)}, u32[]{:S(2)}) copy-start(f32[1,1,2048]{2,1,0:T(1,128)S(1)} %get-tuple-element.30) | copy-start | bytes 24580
  132.8 7.2 %copy-start.21 = (f32[1,1,2048]{2,1,0:T(1,128)}, f32[1,1,2048]{2,1,0:T(1,128)S(1)}, u32[]{:S(2)}) copy-start(f32[1,1,2048]{2,1,0:T(1,128)S(1)} %get-tuple-element.31) | copy-start | bytes 24580
  159.5 22.5 %collective-permute-start.1 = (f32[4,768,90]{1,0,2:T(4,128)S(1)}, f32[4,768,90]{1,0,2:T(4,128)S(1)}, u32[]{:S(2)}, u32[]{:S(2)}) collective-permute-start(f32[4,768,90]{1,0,2:T(4,128)S(1)} %copy.71), channel_id=1, source_target_pairs={{0,1},{1,2},{2,3},{3,4},{4,5},{5,6},{6,7},{7,0},{8,9},{9,10},{10,1... | collective-permute-start | bytes 3317768 | tf_op jit(solution)/shard_map/ppermute | solution.py:13
  164.0 25.0 %collective-permute-start = (f32[4,768,90]{1,0,2:T(4,128)}, f32[4,768,90]{1,0,2:T(4,128)}, u32[]{:S(2)}, u32[]{:S(2)}) collective-permute-start(f32[4,768,90]{1,0,2:T(4,128)} %copy.69), channel_id=1, source_target_pairs={{0,7},{1,0},{2,1},{3,2},{4,3},{5,4},{6,5},{7,6},{8,15},{9,8},{10,9... | collective-permute-start | bytes 3317768 | tf_op jit(solution)/shard_map/ppermute | solution.py:13
  165.1 4.4 %copy-start.10 = (f32[1,1,2048]{2,1,0:T(1,128)S(1)}, f32[1,1,2048]{2,1,0:T(1,128)}, u32[]{:S(2)}) copy-start(f32[1,1,2048]{2,1,0:T(1,128)} %copy-done.9) | copy-start | bytes 24580
  165.1 4.4 %copy-start.18 = (f32[1,1,2048]{2,1,0:T(1,128)S(1)}, f32[1,1,2048]{2,1,0:T(1,128)}, u32[]{:S(2)}) copy-start(f32[1,1,2048]{2,1,0:T(1,128)} %copy-done.17) | copy-start | bytes 24580
  165.1 4.4 %copy-start.20 = (f32[1,1,2048]{2,1,0:T(1,128)S(1)}, f32[1,1,2048]{2,1,0:T(1,128)}, u32[]{:S(2)}) copy-start(f32[1,1,2048]{2,1,0:T(1,128)} %copy-done.19) | copy-start | bytes 24580
  165.1 4.4 %copy-start.22 = (f32[1,1,2048]{2,1,0:T(1,128)S(1)}, f32[1,1,2048]{2,1,0:T(1,128)}, u32[]{:S(2)}) copy-start(f32[1,1,2048]{2,1,0:T(1,128)} %copy-done.21) | copy-start | bytes 24580
  166.3 5.6 %copy-start.12 = (f32[1,1,2048]{2,1,0:T(1,128)S(1)}, f32[1,1,2048]{2,1,0:T(1,128)}, u32[]{:S(2)}) copy-start(f32[1,1,2048]{2,1,0:T(1,128)} %copy-done.11) | copy-start | bytes 24580
  166.3 5.6 %copy-start.14 = (f32[1,1,2048]{2,1,0:T(1,128)S(1)}, f32[1,1,2048]{2,1,0:T(1,128)}, u32[]{:S(2)}) copy-start(f32[1,1,2048]{2,1,0:T(1,128)} %copy-done.13) | copy-start | bytes 24580
  166.3 5.6 %copy-start.16 = (f32[1,1,2048]{2,1,0:T(1,128)S(1)}, f32[1,1,2048]{2,1,0:T(1,128)}, u32[]{:S(2)}) copy-start(f32[1,1,2048]{2,1,0:T(1,128)} %copy-done.15) | copy-start | bytes 24580
  171.8 18.6 %copy-start.7 = (f32[1,4,768,90]{2,3,0,1:T(8,128)S(1)}, f32[1,4,768,90]{2,3,0,1:T(8,128)}, u32[]{:S(2)}) copy-start(f32[1,4,768,90]{2,3,0,1:T(8,128)} %get-tuple-element.21) | copy-start | bytes 3317764
  194.3 4.0 %copy-start.25 = (s32[8192]{0:T(1024)S(1)}, s32[8192]{0:T(1024)}, u32[]{:S(2)}) copy-start(s32[8192]{0:T(1024)} %fusion.4) | copy-start | bytes 98308
  198.3 30.1 %copy-start.26 = (pred[8192]{0:T(1024)(128)(4,1)S(1)}, pred[8192]{0:T(1024)(128)(4,1)}, u32[]{:S(2)}) copy-start(pred[8192]{0:T(1024)(128)(4,1)} %compare_and_fusion.1) | copy-start | bytes 24580
  264.7 5.7 %copy-start.1 = (f32[6,60,2048]{2,1,0:T(8,128)S(1)}, f32[6,60,2048]{2,1,0:T(8,128)}, u32[]{:S(2)}) copy-start(f32[6,60,2048]{2,1,0:T(8,128)} %copy-done) | copy-start | bytes 8847364
  270.4 3.2 %copy-start.3 = (f32[1,60,2048]{2,1,0:T(8,128)S(1)}, f32[1,60,2048]{2,1,0:T(8,128)}, u32[]{:S(2)}) copy-start(f32[1,60,2048]{2,1,0:T(8,128)} %mul.932) | copy-start | bytes 1474564
  270.4 3.2 %copy-start.4 = (f32[1,60,2048]{2,1,0:T(8,128)S(1)}, f32[1,60,2048]{2,1,0:T(8,128)}, u32[]{:S(2)}) copy-start(f32[1,60,2048]{2,1,0:T(8,128)} %mul.939) | copy-start | bytes 1474564
  270.4 3.2 %copy-start.5 = (f32[1,60,2048]{2,1,0:T(8,128)S(1)}, f32[1,60,2048]{2,1,0:T(8,128)}, u32[]{:S(2)}) copy-start(f32[1,60,2048]{2,1,0:T(8,128)} %mul.943) | copy-start | bytes 1474564
  270.4 3.2 %copy-start.8 = (f32[1,60,2048]{2,1,0:T(8,128)S(1)}, f32[1,60,2048]{2,1,0:T(8,128)}, u32[]{:S(2)}) copy-start(f32[1,60,2048]{2,1,0:T(8,128)} %squeeze.134) | copy-start | bytes 1474564
  (5 other events, 8.9 us)
where the time goes:
time: 283 us; the launch traced here: 282 us
  local copies, waits for them, and re-layouts  164 us (58%)
  waiting for transfers between devices  50.2 us (18%)
  other arithmetic  36.3 us (13%)
  matrix products  19.4 us (7%)
  starting transfers between devices  11.1 us (4%)
    gather x2, local copies, waits for them, and re-layouts, local(): jnp.take(face_rows, send_faces, axis=0)  37.2 us
    gather x1, local copies, waits for them, and re-layouts, local(): neighbour = jnp.take(received, recv_faces, axis=0).T  30.1 us
    all_to_all x1, waiting for transfers between devices, local(): lax.all_to_all(outgoing, 'grp', split_axis=1, concat_axis=1, tiled=True)  20.6 us
    slice x4, local copies, waits for them, and re-layouts, face_flux(): jump_h = [far_split[c + 3] - own_split[c + 3] for c in range(3)]  20.5 us
    unnamed x10, other arithmetic  16.7 us
    all_to_all x1, waiting for transfers between devices, across_groups(): lax.all_to_all(outgoing, 'grp', split_axis=1, concat_axis=1, tiled=True)  15.2 us
    ppermute x2, waiting for transfers between devices, shifted(): return lax.ppermute(x, axis, [(i, (i + by) % size) for i in range(size)])  14.4 us
    dot_general x1, matrix products, volume_terms(): jnp.einsum('anm,qms->qans', deriv_mats, coefficients, precision=exact_prec)  10.5 us
  transfers between devices with their start and end apart: 4, of which 4 were waited for; matrix products, arithmetic and copies ran while one was open for 14% of the time, Pallas kernels for 0%

commit v1 on v0

--- a/solution.py
+++ b/solution.py
@@ -105,9 +105,10 @@
     )
     padded = jnp.concatenate([payload, zero_column], 1)
     outgoing = jnp.take(padded, inverse, axis=1).reshape(row_count, groups, capacity)
-    bucket = lax.all_to_all(outgoing, "grp", split_axis=1, concat_axis=1, tiled=True).reshape(
-        row_count, slot_count
-    )
+    bucket = jnp.concatenate(
+        lax.all_to_all(jnp.stack(jnp.split(outgoing, lax.axis_size("grp"), axis=1)), "grp", 0, 0),
+        axis=1,
+    ).reshape(row_count, slot_count)
     node_mask = order_mask(own_group)
     deriv_mats = dmat[0].reshape(3, NPM, NPM) * node_mask[None, :, None] * node_mask[None, None, :]
     trace_mat = tmat[0] * node_mask[None, :]

time: 283 us -> 290 us (1.025); the launches traced: 282 us -> 285 us
    another operation x0 -> x1, other arithmetic: none -> 3.2 us  [local(): jnp.stack(jnp.split(outgoing, lax.axis_size('grp'), axis=1))]
    unnamed x10 -> x11, other arithmetic: 16.7 us -> 17.5 us
    unnamed x70 -> x76, local copies, waits for them, and re-layouts: 6.34 us -> 5.64 us
  transfers between devices with their start and end apart: 4 -> 4, of which waited for: 4 -> 4; matrix products, arithmetic and copies ran while one was open for 14% -> 13% of each run, Pallas kernels for 0% -> 0%
where the time goes in v1:
time: 290 us; the launch traced here: 285 us
  local copies, waits for them, and re-layouts  164 us (57%)
  waiting for transfers between devices  50.1 us (17%)
  other arithmetic  37.9 us (13%)
  matrix products  19.4 us (7%)
  starting transfers between devices  11.9 us (4%)
    gather x2, local copies, waits for them, and re-layouts, local(): jnp.take(face_rows, send_faces, axis=0)  37.2 us
    gather x1, local copies, waits for them, and re-layouts, local(): neighbour = jnp.take(received, recv_faces, axis=0).T  30 us
    slice x4, local copies, waits for them, and re-layouts, face_flux(): jump_h = [far_split[c + 3] - own_split[c + 3] for c in range(3)]  20.7 us
    all_to_all x1, waiting for transfers between devices, local(): lax.all_to_all(jnp.stack(jnp.split(outgoing, lax.axis_size('grp'), axis=1...  20 us
    unnamed x11, other arithmetic  17.5 us
    all_to_all x1, waiting for transfers between devices, across_groups(): lax.all_to_all(outgoing, 'grp', split_axis=1, concat_axis=1, tiled=True)  15.5 us
    ppermute x2, waiting for transfers between devices, shifted(): return lax.ppermute(x, axis, [(i, (i + by) % size) for i in range(size)])  14.5 us
    dot_general x1, matrix products, volume_terms(): jnp.einsum('anm,qms->qans', deriv_mats, coefficients, precision=exact_prec)  10.5 us
  transfers between devices with their start and end apart: 4, of which 4 were waited for; matrix products, arithmetic and copies ran while one was open for 13% of the time, Pallas kernels for 0%

profile of v1, /device:TPU:1, one launch (start us, length us, event | category | flops | bytes accessed | tf_op | source)
XLA Modules:
  0.0 284.6 jit_solution(8667546582597997317)
XLA Ops:
  0.7 4.3 %scatter_custom_fusion = s32[2048]{0:T(1024)S(1)} fusion(s32[1024]{0:T(1024)S(1)} %compare_select_fusion.3, s32[1024]{0:T(1024)S(1)} %iota.14, s32[]{:T(128)} %constant.33.clone.1), kind=kCustom, calls=%fused_computation.89 | custom fusion | bytes 8196 | tf_op jit(solution)/shard_map/scatter | solution.py:104
  10.5 6.6 %gather_fusion = f32[2048,235]{1,0:T(8,128)S(1)} fusion(f32[235,1025]{0,1:T(8,128)S(1)} %select_maximum_fusion, s32[2048]{0:T(1024)S(1)} %fusion.12), kind=kCustom, calls=%fused_computation | custom fusion | bytes 3858432 | tf_op jit(solution)/shard_map/jit(_take)/gather | solution.py:107
  22.4 3.2 %pad_maximum_fusion.1 = f32[4,235,1,512]{3,2,1,0:T(1,128)} fusion(f32[1,235,1,512]{3,2,1,0:T(1,128)S(1)} %get-tuple-element.27, f32[1,235,1,512]{3,2,1,0:T(1,128)S(1)} %get-tuple-element.28, f32[1,235,1,512]{3,2,1,0:T(1,128)S(1)} %get-tuple-element.29, f32[1,235,1,512]{3,2,1,0:T(1,128)S(1)} %get-tuple-element.26), kind=kLoop, calls=%fused_computation.11 | loop fusion | flops 1443840 | bytes 3850240 | tf_op jit(solution)/shard_map/stack | solution.py:109
  25.6 4.7 %all-to-all-start = ((f32[4,235,1,512]{3,2,1,0:T(1,128)}), f32[4,235,1,512]{3,2,1,0:T(1,128)S(1)}, u32[]{:S(2)}, u32[]{:S(2)}) async-start(f32[4,235,1,512]{3,2,1,0:T(1,128)} %pad_maximum_fusion.1), calls=%async_computation | async-start | bytes 3850240 | tf_op jit(solution)/shard_map/all_to_all | solution.py:109
  32.8 20.0 %all-to-all-done = f32[4,235,1,512]{3,2,1,0:T(1,128)S(1)} async-done(((f32[4,235,1,512]{3,2,1,0:T(1,128)}), f32[4,235,1,512]{3,2,1,0:T(1,128)S(1)}, u32[]{:S(2)}, u32[]{:S(2)}) %all-to-all-start) | async-done | bytes 1925152 | tf_op jit(solution)/shard_map/all_to_all | solution.py:109
  55.0 2.5 reshape.2023
  57.5 2.5 reshape.2063
  59.9 4.7 %convolution_bitcast_fusion.1 = f32[6,60,2048]{2,1,0:T(8,128)S(1)} fusion(f32[6,35,2048]{2,1,0:T(8,128)} %reshape.2023, f32[1,60,35]{1,0,2:T(1,128)S(1)} %broadcast_multiply_fusion), kind=kOutput, calls=%fused_computation.7 | convolution fusion | flops 309657600 | bytes 4677840 | tf_op jit(solution)/shard_map/pm,qms->qps/dot_general | solution.py:117
  64.6 3.0 %reshape.2024 = f32[90,8192]{1,0:T(8,128)} reshape(f32[6,60,2048]{2,1,0:T(8,128)S(1)} %convolution_bitcast_fusion.1) | data formatting | bytes 5898240 | tf_op jit(solution)/shard_map/reshape | solution.py:117
  67.6 5.2 %copy.142 = f32[90,8192]{0,1:T(8,128)} copy(f32[90,8192]{1,0:T(8,128)} %reshape.2024) | data formatting | bytes 5898240 | tf_op jit(solution)/shard_map/reshape | solution.py:117
  72.8 3.8 %concatenate.15 = f32[8193,90]{1,0:T(8,128)} pad(f32[8192,90]{1,0:T(8,128)} %bitcast.203, f32[]{:T(128)} %constant.45.clone.1), padding=0_1x0_0 | pad | bytes 5898604 | tf_op jit(solution)/shard_map/concatenate | solution.py:120
  76.6 33.3 %gather_fusion.1 = f32[9216,90]{1,0:T(8,128)} fusion(f32[8193,90]{1,0:T(8,128)} %concatenate.15, s32[9216]{0:T(1024)S(1)} %fusion.4), kind=kCustom, calls=%fused_computation.1 | custom fusion | bytes 6672384 | tf_op jit(solution)/shard_map/jit(_take)/gather | solution.py:123
  109.9 3.9 %copy.143 = f32[3,4,768,90]{2,3,0,1:T(8,128)S(1)} copy(f32[3,4,768,90]{3,2,1,0:T(8,128)} %bitcast.201) | data formatting | bytes 6635520 | tf_op jit(solution)/shard_map/jit(_take)/gather | solution.py:123
  116.0 4.3 %all-to-all-start.1 = ((f32[3,4,768,90]{2,3,0,1:T(8,128)}), f32[3,4,768,90]{2,3,0,1:T(8,128)S(1)}, u32[]{:S(2)}, u32[]{:S(2)}) async-start(f32[3,4,768,90]{2,3,0,1:T(8,128)} %broadcast_select_fusion), calls=%async_computation.1 | async-start | bytes 7077888 | tf_op jit(solution)/shard_map/all_to_all | solution.py:82
  120.3 10.5 %convolution_bitcast_fusion = f32[6,3,35,2048]{3,2,1,0:T(8,128)} fusion(f32[6,35,2048,1]{2,1,0,3:T(8,128)} %reshape.2063, f32[3,35,35]{2,1,0:T(8,128)} %copy.140), kind=kOutput, calls=%fused_computation.5 | convolution fusion | flops 541900800 | bytes 6895980 | tf_op jit(solution)/shard_map/anm,qms->qans/dot_general | solution.py:30
  144.6 15.5 %all-to-all-done.1 = f32[3,4,768,90]{2,3,0,1:T(8,128)S(1)} async-done(((f32[3,4,768,90]{2,3,0,1:T(8,128)}), f32[3,4,768,90]{2,3,0,1:T(8,128)S(1)}, u32[]{:S(2)}, u32[]{:S(2)}) %all-to-all-start.1) | async-done | bytes 3317792 | tf_op jit(solution)/shard_map/all_to_all | solution.py:82
  162.0 2.8 collective-permute-start.1
  176.7 7.9 %collective-permute-done.1 = f32[4,768,90]{1,0,2:T(4,128)S(1)} collective-permute-done((f32[4,768,90]{1,0,2:T(4,128)S(1)}, f32[4,768,90]{1,0,2:T(4,128)S(1)}, u32[]{:S(2)}, u32[]{:S(2)}) %collective-permute-start.1) | collective-permute-done | bytes 1105952 | tf_op jit(solution)/shard_map/ppermute | solution.py:13
  184.8 6.6 %collective-permute-done = f32[4,768,90]{1,0,2:T(4,128)} collective-permute-done((f32[4,768,90]{1,0,2:T(4,128)}, f32[4,768,90]{1,0,2:T(4,128)}, u32[]{:S(2)}, u32[]{:S(2)}) %collective-permute-start) | collective-permute-done | bytes 1105952 | tf_op jit(solution)/shard_map/ppermute | solution.py:13
  193.2 3.6 %copy.148 = f32[3,4,768,90]{3,2,1,0:T(8,128)} copy(f32[3,4,768,90]{2,3,0,1:T(8,128)S(1)} %pad_maximum_fusion) | data formatting | bytes 6635520 | tf_op jit(solution)/shard_map/stack | solution.py:88
  196.8 4.0 %concatenate.16 = f32[9217,90]{1,0:T(8,128)} pad(f32[9216,90]{1,0:T(8,128)} %bitcast.202, f32[]{:T(128)} %constant.45.clone.1), padding=0_1x0_0 | pad | bytes 6635884 | tf_op jit(solution)/shard_map/concatenate | solution.py:125
  200.7 30.0 %gather_fusion.2 = f32[8192,90]{1,0:T(8,128)} fusion(f32[9217,90]{1,0:T(8,128)} %concatenate.16, s32[8192]{0:T(1024)S(1)} %copy-done.25), kind=kCustom, calls=%fused_computation.2 | custom fusion | bytes 5931008 | tf_op jit(solution)/shard_map/jit(_take)/gather | solution.py:128
  230.8 6.2 %select_bitcast_fusion = f32[90,8192]{0,1:T(8,128)S(1)} fusion(f32[8192,90]{1,0:T(8,128)} %gather_fusion.2, pred[8192]{0:T(1024)(128)(4,1)S(1)} %copy-done.27), kind=kLoop, calls=%fused_computation.4 | loop fusion | flops 737280 | bytes 5906432 | tf_op jit(solution)/shard_map/jit(_take)/select_n | solution.py:128
  237.0 11.1 %fusion.15 = (f32[15,8192]{0,1:T(8,128)}, f32[15,8192]{0,1:T(8,128)}, f32[15,8192]{0,1:T(8,128)}, f32[15,8192]{0,1:T(8,128)}, f32[15,8192]{0,1:T(8,128)}, /*index=5*/f32[15,8192]{0,1:T(8,128)}) fusion(f32[90,8192]{0,1:T(8,128)S(1)} %select_bitcast_fusion), kind=kLoop, calls=%fused_computation.92 | loop fusion | bytes 5898240 | tf_op jit(solution)/shard_map/slice | solution.py:56
  248.1 2.8 copy.149
  251.9 2.8 copy.150
  255.7 2.8 copy.151
  259.5 2.8 copy.152
  263.3 2.8 copy.153
  267.1 3.9 %copy.154 = f32[15,8192]{1,0:T(8,128)} copy(f32[15,8192]{0,1:T(8,128)} %get-tuple-element.13) | data formatting | bytes 983040 | tf_op jit(solution)/shard_map/slice | solution.py:56
  273.1 3.2 %multiply_dynamic-update-slice_fusion.5 = (f32[6,60,2048]{2,1,0:T(8,128)S(1)}, f32[1,60,2048]{2,1,0:T(8,128)S(1)}, f32[1,60,2048]{2,1,0:T(8,128)S(1)}, f32[1,60,...) fusion(f32[1,60,2048]{2,1,0:T(8,128)} %mul.929, f32[1,60,2048]{2,1,0:T(8,128)} %mul.943, ...), kind=kLoop, calls=%fused_computation.35 | loop fusion | flops 2088959 | bytes 10027008
  278.7 4.2 %fusion = f32[6,35,2048]{2,1,0:T(8,128)S(1)} fusion(f32[6,35,2048]{2,1,0:T(8,128)} %negate_dynamic-update-slice_fusion, f32[6,60,2048]{2,1,0:T(8,128)S(1)} %multiply_dynamic-update-slice_fusion, f32[1,35,60]{2,0,1:T(1,128)S(1)} %copy-done.28, f32[35]{0:T(128)S(1)} %copy-done.33), kind=kOutput, calls=%fused_computation.9 | convolution fusion | flops 310089792 | bytes 6398300 | tf_op jit(solution)/shard_map/mp,qps->qms/dot_general | solution.py:77
  (138 shorter events, 58.2 us)
Async XLA Ops:
  0.0 7.7 %copy-start.26 = (f32[12,1024]{1,0:T(8,128)S(1)}, f32[12,1024]{1,0:T(8,128)}, u32[]{:S(2)}) copy-start(f32[12,1024]{1,0:T(8,128)} %param.13) | copy-start | bytes 147460
  0.0 7.9 %copy-start.31 = (f32[4,1024]{1,0:T(4,128)S(1)}, f32[4,1024]{1,0:T(4,128)}, u32[]{:S(2)}) copy-start(f32[4,1024]{1,0:T(4,128)} %param.14) | copy-start | bytes 49156
  25.6 4.7 %copy-start.23 = (s32[9216]{0:T(1024)S(1)}, s32[9216]{0:T(1024)}, u32[]{:S(2)}) copy-start(s32[9216]{0:T(1024)} %param.17) | copy-start | bytes 110596
  25.6 4.9 %copy-start.29 = (f32[1,105,35]{1,0,2:T(1,128)S(1)}, f32[1,105,35]{1,0,2:T(1,128)}, u32[]{:S(2)}) copy-start(f32[1,105,35]{1,0,2:T(1,128)} %param.19) | copy-start | bytes 44104
  25.6 5.9 %copy-start.30 = (f32[1,60,35]{1,0,2:T(1,128)S(1)}, f32[1,60,35]{1,0,2:T(1,128)}, u32[]{:S(2)}) copy-start(f32[1,60,35]{1,0,2:T(1,128)} %param.20) | copy-start | bytes 25204
  25.6 6.0 %copy-start.24 = (s32[8192]{0:T(1024)S(1)}, s32[8192]{0:T(1024)}, u32[]{:S(2)}) copy-start(s32[8192]{0:T(1024)} %param.18) | copy-start | bytes 98308
  25.6 27.2 %all-to-all-start = ((f32[4,235,1,512]{3,2,1,0:T(1,128)}), f32[4,235,1,512]{3,2,1,0:T(1,128)S(1)}, u32[]{:S(2)}, u32[]{:S(2)}) async-start(f32[4,235,1,512]{3,2,1,0:T(1,128)} %pad_maximum_fusion.1), calls=%async_computation | async-start | bytes 3850240 | tf_op jit(solution)/shard_map/all_to_all | solution.py:109
  30.4 22.9 %copy-start.32 = (f32[35]{0:T(128)}, f32[35]{0:T(128)S(1)}, u32[]{:S(2)}) copy-start(f32[35]{0:T(128)S(1)} %compare_convert_fusion) | copy-start | bytes 424
  116.0 44.1 %all-to-all-start.1 = ((f32[3,4,768,90]{2,3,0,1:T(8,128)}), f32[3,4,768,90]{2,3,0,1:T(8,128)S(1)}, u32[]{:S(2)}, u32[]{:S(2)}) async-start(f32[3,4,768,90]{2,3,0,1:T(8,128)} %broadcast_select_fusion), calls=%async_computation.1 | async-start | bytes 7077888 | tf_op jit(solution)/shard_map/all_to_all | solution.py:82
  134.9 4.8 %copy-start.9 = (f32[1,1,2048]{2,1,0:T(1,128)}, f32[1,1,2048]{2,1,0:T(1,128)S(1)}, u32[]{:S(2)}) copy-start(f32[1,1,2048]{2,1,0:T(1,128)S(1)} %get-tuple-element.32) | copy-start | bytes 24580
  134.9 7.2 %copy-start.11 = (f32[1,1,2048]{2,1,0:T(1,128)}, f32[1,1,2048]{2,1,0:T(1,128)S(1)}, u32[]{:S(2)}) copy-start(f32[1,1,2048]{2,1,0:T(1,128)S(1)} %get-tuple-element.36) | copy-start | bytes 24580
  134.9 7.2 %copy-start.13 = (f32[1,1,2048]{2,1,0:T(1,128)}, f32[1,1,2048]{2,1,0:T(1,128)S(1)}, u32[]{:S(2)}) copy-start(f32[1,1,2048]{2,1,0:T(1,128)S(1)} %get-tuple-element.37) | copy-start | bytes 24580
  134.9 7.2 %copy-start.15 = (f32[1,1,2048]{2,1,0:T(1,128)}, f32[1,1,2048]{2,1,0:T(1,128)S(1)}, u32[]{:S(2)}) copy-start(f32[1,1,2048]{2,1,0:T(1,128)S(1)} %get-tuple-element.38) | copy-start | bytes 24580
  135.0 7.2 %copy-start.17 = (f32[1,1,2048]{2,1,0:T(1,128)}, f32[1,1,2048]{2,1,0:T(1,128)S(1)}, u32[]{:S(2)}) copy-start(f32[1,1,2048]{2,1,0:T(1,128)S(1)} %get-tuple-element.33) | copy-start | bytes 24580
  135.0 7.2 %copy-start.19 = (f32[1,1,2048]{2,1,0:T(1,128)}, f32[1,1,2048]{2,1,0:T(1,128)S(1)}, u32[]{:S(2)}) copy-start(f32[1,1,2048]{2,1,0:T(1,128)S(1)} %get-tuple-element.34) | copy-start | bytes 24580
  135.0 7.2 %copy-start.21 = (f32[1,1,2048]{2,1,0:T(1,128)}, f32[1,1,2048]{2,1,0:T(1,128)S(1)}, u32[]{:S(2)}) copy-start(f32[1,1,2048]{2,1,0:T(1,128)S(1)} %get-tuple-element.35) | copy-start | bytes 24580
  162.0 22.5 %collective-permute-start.1 = (f32[4,768,90]{1,0,2:T(4,128)S(1)}, f32[4,768,90]{1,0,2:T(4,128)S(1)}, u32[]{:S(2)}, u32[]{:S(2)}) collective-permute-start(f32[4,768,90]{1,0,2:T(4,128)S(1)} %copy.146), channel_id=1, source_target_pairs={{0,1},{1,2},{2,3},{3,4},{4,5},{5,6},{6,7},{7,0},{8,9},{9,10},{10,1... | collective-permute-start | bytes 3317768 | tf_op jit(solution)/shard_map/ppermute | solution.py:13
  166.5 24.9 %collective-permute-start = (f32[4,768,90]{1,0,2:T(4,128)}, f32[4,768,90]{1,0,2:T(4,128)}, u32[]{:S(2)}, u32[]{:S(2)}) collective-permute-start(f32[4,768,90]{1,0,2:T(4,128)} %copy.144), channel_id=1, source_target_pairs={{0,7},{1,0},{2,1},{3,2},{4,3},{5,4},{6,5},{7,6},{8,15},{9,8},{10,9... | collective-permute-start | bytes 3317768 | tf_op jit(solution)/shard_map/ppermute | solution.py:13
  168.7 3.2 %copy-start.10 = (f32[1,1,2048]{2,1,0:T(1,128)S(1)}, f32[1,1,2048]{2,1,0:T(1,128)}, u32[]{:S(2)}) copy-start(f32[1,1,2048]{2,1,0:T(1,128)} %copy-done.9) | copy-start | bytes 24580
  168.7 3.2 %copy-start.18 = (f32[1,1,2048]{2,1,0:T(1,128)S(1)}, f32[1,1,2048]{2,1,0:T(1,128)}, u32[]{:S(2)}) copy-start(f32[1,1,2048]{2,1,0:T(1,128)} %copy-done.17) | copy-start | bytes 24580
  168.7 3.2 %copy-start.20 = (f32[1,1,2048]{2,1,0:T(1,128)S(1)}, f32[1,1,2048]{2,1,0:T(1,128)}, u32[]{:S(2)}) copy-start(f32[1,1,2048]{2,1,0:T(1,128)} %copy-done.19) | copy-start | bytes 24580
  170.8 3.5 %copy-start.12 = (f32[1,1,2048]{2,1,0:T(1,128)S(1)}, f32[1,1,2048]{2,1,0:T(1,128)}, u32[]{:S(2)}) copy-start(f32[1,1,2048]{2,1,0:T(1,128)} %copy-done.11) | copy-start | bytes 24580
  170.8 3.5 %copy-start.14 = (f32[1,1,2048]{2,1,0:T(1,128)S(1)}, f32[1,1,2048]{2,1,0:T(1,128)}, u32[]{:S(2)}) copy-start(f32[1,1,2048]{2,1,0:T(1,128)} %copy-done.13) | copy-start | bytes 24580
  170.8 3.5 %copy-start.16 = (f32[1,1,2048]{2,1,0:T(1,128)S(1)}, f32[1,1,2048]{2,1,0:T(1,128)}, u32[]{:S(2)}) copy-start(f32[1,1,2048]{2,1,0:T(1,128)} %copy-done.15) | copy-start | bytes 24580
  176.7 16.2 %copy-start.7 = (f32[1,4,768,90]{2,3,0,1:T(8,128)S(1)}, f32[1,4,768,90]{2,3,0,1:T(8,128)}, u32[]{:S(2)}) copy-start(f32[1,4,768,90]{2,3,0,1:T(8,128)} %get-tuple-element.21) | copy-start | bytes 3317764
  196.8 4.0 %copy-start.25 = (s32[8192]{0:T(1024)S(1)}, s32[8192]{0:T(1024)}, u32[]{:S(2)}) copy-start(s32[8192]{0:T(1024)} %fusion.5) | copy-start | bytes 98308
  200.7 30.0 %copy-start.27 = (pred[8192]{0:T(1024)(128)(4,1)S(1)}, pred[8192]{0:T(1024)(128)(4,1)}, u32[]{:S(2)}) copy-start(pred[8192]{0:T(1024)(128)(4,1)} %compare_and_fusion.1) | copy-start | bytes 24580
  267.1 5.9 %copy-start.1 = (f32[6,60,2048]{2,1,0:T(8,128)S(1)}, f32[6,60,2048]{2,1,0:T(8,128)}, u32[]{:S(2)}) copy-start(f32[6,60,2048]{2,1,0:T(8,128)} %copy-done) | copy-start | bytes 8847364
  273.0 3.2 %copy-start.3 = (f32[1,60,2048]{2,1,0:T(8,128)S(1)}, f32[1,60,2048]{2,1,0:T(8,128)}, u32[]{:S(2)}) copy-start(f32[1,60,2048]{2,1,0:T(8,128)} %mul.932) | copy-start | bytes 1474564
  273.0 3.2 %copy-start.4 = (f32[1,60,2048]{2,1,0:T(8,128)S(1)}, f32[1,60,2048]{2,1,0:T(8,128)}, u32[]{:S(2)}) copy-start(f32[1,60,2048]{2,1,0:T(8,128)} %mul.939) | copy-start | bytes 1474564
  273.0 3.2 %copy-start.5 = (f32[1,60,2048]{2,1,0:T(8,128)S(1)}, f32[1,60,2048]{2,1,0:T(8,128)}, u32[]{:S(2)}) copy-start(f32[1,60,2048]{2,1,0:T(8,128)} %mul.943) | copy-start | bytes 1474564
  273.1 3.2 %copy-start.8 = (f32[1,60,2048]{2,1,0:T(8,128)S(1)}, f32[1,60,2048]{2,1,0:T(8,128)}, u32[]{:S(2)}) copy-start(f32[1,60,2048]{2,1,0:T(8,128)} %squeeze.134) | copy-start | bytes 1474564
  (6 other events, 12.2 us)
